TPU v7x, 32 devices: a whole 2x2x4 slice. The times are simulated.
32 devices in a mesh: gx: 4 (over x, core), gy: 8 (over z, y).
Axes of the slice: x: 2, y: 2, z: 4, core: 2. Of those that a mesh axis runs over, the one named last changes fastest.
Arguments:
- mask_feats: bfloat16 [64, 8, 14, 14, 256], P(('gx', 'gy')), may hold values from -6 to 6
- mask_cot: bfloat16 [64, 8, 14, 14, 256], P(('gx', 'gy')), may hold values from -6 to 6
- roi_counts: int32 [64], P(('gx', 'gy')), may hold values from 1 to 8, as said below
- rpn_feats: bfloat16 [64, 48, 32, 256], P(('gx', 'gy')), may hold values from -6 to 6
- rpn_cot: bfloat16 [64, 48, 32, 256], P(('gx', 'gy')), may hold values from -360 to 360
- anchor_counts: int32 [64], P(('gx', 'gy')), may hold values from 32 to 223
- mask_weight: float32 [2304, 256], replicated, may hold values from -0.125 to 0.125
- rpn_weight: float32 [2304, 256], replicated, may hold values from -0.125 to 0.125
- mask_moment: float32 [2304, 256], replicated, may hold values from -6 to 6
- rpn_moment: float32 [2304, 256], replicated, may hold values from -6 to 6
Outputs:
- new_mask_weight: float32 [2304, 256], replicated
- new_rpn_weight: float32 [2304, 256], replicated
- new_mask_moment: float32 [2304, 256], replicated
- new_rpn_moment: float32 [2304, 256], replicated
Inputs may be any that keep to these rules, and one draw needn't show every extreme that they name: `roi_counts`: every image has at least one positive ROI; some image has all 8 slots positive.
All inputs are finite; a program needn't handle non-finite values.
Results may differ from a plain program's by a relative error of at most 0.0003.
Values sent between devices are 32-bit elements; how exact they have to be, the bound alone decides.
A program may use at most 128 MiB of HBM per device.

v0:
```python
import jax
import jax.numpy as jnp
from jax import lax
from jax.sharding import PartitionSpec as P


def weight_grad(feats, cotan):
    grid_rows = feats.shape[1]
    grid_cols = feats.shape[2]
    chans = feats.shape[3]
    padded = jnp.pad(feats, ((0, 0), (1, 1), (1, 1), (0, 0)))
    flat_cot = cotan.reshape(-1, chans)
    blocks = []
    for row_tap in range(3):
        for col_tap in range(3):
            window = padded[
                :, row_tap : row_tap + grid_rows, col_tap : col_tap + grid_cols, :
            ].reshape(-1, chans)
            blocks.append(
                lax.dot_general(
                    window, flat_cot, (((0,), (0,)), ((), ())), preferred_element_type=jnp.float32
                )
            )
    return jnp.concatenate(blocks, axis=0)


def step_update(weight, moment, grad):
    fresh_moment = 0.9 * moment + grad
    return (weight - 0.02 * fresh_moment, fresh_moment)


def on_device(
    mask_feats,
    mask_cot,
    roi_counts,
    rpn_feats,
    rpn_cot,
    anchor_counts,
    mask_weight,
    rpn_weight,
    mask_moment,
    rpn_moment,
):
    slot_count = mask_feats.shape[1]
    side = mask_feats.shape[2]
    chans = mask_feats.shape[4]
    slots = jnp.arange(slot_count, dtype=jnp.int32)
    valid_slots = (slots[None, :] < roi_counts[:, None]).astype(jnp.bfloat16)
    masked = mask_cot * valid_slots[:, :, None, None, None]
    mask_local = weight_grad(
        mask_feats.reshape(-1, side, side, chans), masked.reshape(-1, side, side, chans)
    )
    rpn_local = weight_grad(rpn_feats, rpn_cot)
    local_counts = jnp.stack([jnp.sum(roi_counts), jnp.sum(anchor_counts)]).astype(jnp.float32)
    mask_sum, rpn_sum, totals = lax.psum((mask_local, rpn_local, local_counts), ("gx", "gy"))
    mask_grad = mask_sum / totals[0]
    rpn_grad = rpn_sum / totals[1]
    new_mask_weight, new_mask_moment = step_update(mask_weight, mask_moment, mask_grad)
    new_rpn_weight, new_rpn_moment = step_update(rpn_weight, rpn_moment, rpn_grad)
    return (new_mask_weight, new_rpn_weight, new_mask_moment, new_rpn_moment)


def solution(mesh):
    placed = (
        P(("gx", "gy"), None, None, None, None),
        P(("gx", "gy"), None, None, None, None),
        P(("gx", "gy")),
        P(("gx", "gy"), None, None, None),
        P(("gx", "gy"), None, None, None),
        P(("gx", "gy")),
        P(),
        P(),
        P(),
        P(),
    )
    return jax.shard_map(
        on_device, mesh=mesh, in_specs=placed, out_specs=(P(), P(), P(), P()), check_vma=False
    )
```

profile of v0, /device:TPU:1, one launch (start us, length us, event | category | flops | bytes accessed | tf_op | source)
XLA Modules:
  0.0 256.8 jit_solution(18293968853926520437)
XLA Ops:
  7.2 0.0 copy-start
  7.2 0.0 all-reduce.5.cloned.1.call-start
  7.2 0.8 compare_convert_fusion
  8.1 1.6 broadcast_multiply_fusion
  9.7 1.6 copy.29
  11.3 3.7 %reshape_reshape.3 = bf16[3136,256]{1,0:T(8,128)(2,1)} reshape(bf16[2,8,14,14,256]{4,3,2,1,0:T(8,128)(2,1)} %copy.29) | data formatting | bytes 3211264 | tf_op jit(solution)/shard_map/reshape;reshape | solution.py:12
  15.0 1.6 copy.81
  16.5 4.3 %pad_slice_fusion = (bf16[16,14,14,256]{3,0,2,1:T(8,128)(2,1)}, bf16[16,14,14,256]{3,0,2,1:T(8,128)(2,1)}, bf16[16,14,14,256]{3,0,2,1:T(8,128)(2,1)}, bf16[16,14...) fusion(bf16[16,14,14,256]{3,0,2,1:T(8,128)(2,1)S(1)} %bitcast.89), kind=kLoop, calls=%fused_computation.4 | loop fusion | bytes 14450688 | tf_op jit(solution)/shard_map/slice | solution.py:16
  20.8 1.8 copy.28
  22.7 3.6 %reshape.70 = bf16[3136,256]{1,0:T(8,128)(2,1)} reshape(bf16[16,14,14,256]{3,2,1,0:T(8,128)(2,1)} %copy.28) | data formatting | bytes 3211264 | tf_op jit(solution)/shard_map/reshape | solution.py:18
  26.3 3.3 %copy.30 = bf16[16,14,14,256]{3,2,1,0:T(8,128)(2,1)} copy(bf16[16,14,14,256]{3,0,2,1:T(8,128)(2,1)} %get-tuple-element.11) | data formatting | bytes 3211264 | tf_op jit(solution)/shard_map/slice | solution.py:16
  29.6 3.6 %reshape.71 = bf16[3136,256]{1,0:T(8,128)(2,1)} reshape(bf16[16,14,14,256]{3,2,1,0:T(8,128)(2,1)} %copy.30) | data formatting | bytes 3211264 | tf_op jit(solution)/shard_map/reshape | solution.py:18
  33.2 3.3 %copy.31 = bf16[16,14,14,256]{3,2,1,0:T(8,128)(2,1)} copy(bf16[16,14,14,256]{3,0,2,1:T(8,128)(2,1)} %get-tuple-element.12) | data formatting | bytes 3211264 | tf_op jit(solution)/shard_map/slice | solution.py:16
  36.5 3.6 %reshape.72 = bf16[3136,256]{1,0:T(8,128)(2,1)} reshape(bf16[16,14,14,256]{3,2,1,0:T(8,128)(2,1)} %copy.31) | data formatting | bytes 3211264 | tf_op jit(solution)/shard_map/reshape | solution.py:18
  40.1 3.3 %copy.32 = bf16[16,14,14,256]{3,2,1,0:T(8,128)(2,1)} copy(bf16[16,14,14,256]{3,0,2,1:T(8,128)(2,1)} %get-tuple-element.13) | data formatting | bytes 3211264 | tf_op jit(solution)/shard_map/slice | solution.py:16
  43.3 3.6 %reshape.73 = bf16[3136,256]{1,0:T(8,128)(2,1)} reshape(bf16[16,14,14,256]{3,2,1,0:T(8,128)(2,1)} %copy.32) | data formatting | bytes 3211264 | tf_op jit(solution)/shard_map/reshape | solution.py:18
  47.0 3.4 %convolution_dynamic-update-slice_fusion.7 = f32[2304,256]{1,0:T(8,128)} fusion(bf16[3136,256]{1,0:T(8,128)(2,1)} %reshape.70, bf16[3136,256]{1,0:T(8,128)(2,1)} %reshape_reshape.3), kind=kOutput, calls=%fused_computation.36 | convolution fusion | flops 411041792 | bytes 3473408 | tf_op jit(solution)/shard_map/dot_general | solution.py:20
  50.4 1.4 convolution_dynamic-update-slice_fusion.6
  51.8 0.1 copy-done.12
  51.8 1.3 convolution_dynamic-update-slice_fusion.5
  53.2 0.1 copy-done.13
  53.2 1.3 convolution_dynamic-update-slice_fusion.4
  54.6 0.1 copy-done.2
  54.7 1.5 fusion.25
  56.2 0.6 copy.35
  56.8 1.4 reshape.74
  58.2 2.0 copy.36
  60.2 1.4 reshape.75
  61.6 2.0 copy.37
  63.6 1.4 reshape.76
  65.0 2.0 copy.38
  67.1 1.4 reshape.77
  68.5 2.3 copy.39
  70.8 1.8 fusion.24
  72.6 2.1 fusion.22
  74.7 2.0 fusion.20
  76.7 0.0 copy-start.3
  76.7 1.3 fusion.18
  78.1 0.1 copy-done.3
  78.1 0.6 fusion.8
  78.8 1.3 fusion.16
  80.1 2.1 fusion.14
  82.2 2.3 fusion.12
  84.5 0.0 copy-start.7
  84.5 2.1 fusion.10
  86.6 0.0 copy-start.4
  86.6 0.0 copy-start.8
  86.6 1.3 convolution_dynamic-update-slice_fusion.3
  88.0 0.1 copy-done.4
  88.1 0.9 copy-done.8
  89.0 1.4 convolution_dynamic-update-slice_fusion.2
  90.3 0.1 copy-done.9
  90.4 1.4 convolution_dynamic-update-slice_fusion.1
  91.8 0.0 copy-done.10
  91.8 1.4 convolution_dynamic-update-slice_fusion
  93.2 0.0 all-reduce.5.cloned.1.call-update
  93.2 0.6 copy-done.14
  93.8 0.6 reduce_sum.18
  94.5 0.6 reduce_sum.19
  95.1 1.4 add_convert_fusion
  96.5 40.9 %psum.22 = f32[2]{0:T(128)S(1)} all-reduce(f32[2]{0:T(128)S(1)} %add_convert_fusion), channel_id=1, replica_groups=mesh['gx'=4,'gy'=8] {'gx','gy'}, use_global_device_ids=true, to_apply=%region_3.4 | all-reduce | flops 2 | bytes 16 | tf_op jit(solution)/shard_map/psum | solution.py:55
  137.3 0.7 fusion.42
  138.0 101.4 %all-reduce.5.cloned.1.call-done = (f32[2304,256]{1,0:T(8,128)}, f32[2304,256]{1,0:T(8,128)}) async-done(((f32[2304,256]{1,0:T(8,128)}, f32[2304,256]{1,0:T(8,128)}), (f32[2304,256]{1,0:T(8,128)}, f32[2304,256]{1,0:T(8,128)})) %all-reduce.5.cloned.1.call-update) | async-done | bytes 4718608 | tf_op jit(solution)/shard_map/psum | solution.py:55
  239.4 10.6 %multiply_subtract_fusion = (f32[2304,256]{1,0:T(8,128)}, f32[2304,256]{1,0:T(8,128)}, f32[2304,256]{1,0:T(8,128)}, f32[2304,256]{1,0:T(8,128)}) fusion(f32[2304,256]{1,0:T(8,128)} %param.17, f32[2304,256]{1,0:T(8,128)} %get-tuple-element.5, f32[]{:T(128)} %bitcast.25, f32[2304,256]{1,0:T(8,128)} %param.19, f32[2304,256]{1,0:T(8,128)} %param.16, ...), kind=kLoop, calls=%fused_computation | loop fusion | flops 5898240 | bytes 23592968 | tf_op jit(solution)/shard_map/sub | solution.py:29
  (18 shorter events, 0.0 us)
Async XLA Ops:
  7.2 63.6 %copy-start = (bf16[2,48,32,256]{3,2,1,0:T(8,128)(2,1)S(1)}, bf16[2,48,32,256]{3,2,1,0:T(8,128)(2,1)}, u32[]{:S(2)}) copy-start(bf16[2,48,32,256]{3,2,1,0:T(8,128)(2,1)} %param.14) | copy-start | bytes 4718596
  7.2 232.3 %all-reduce.5.cloned.1.call-start = ((), (), s32[]{:S(2)}) async-start(), calls=%async_computation | async-start | bytes 9437184 | tf_op jit(solution)/shard_map/psum | solution.py:55
  47.0 3.4 %copy-start.5 = (bf16[3136,256]{1,0:T(8,128)(2,1)S(1)}, bf16[3136,256]{1,0:T(8,128)(2,1)}, u32[]{:S(2)}) copy-start(bf16[3136,256]{1,0:T(8,128)(2,1)} %reshape_reshape.3) | copy-start | bytes 4816900
  47.0 3.4 %copy-start.11 = (bf16[3136,256]{1,0:T(8,128)(2,1)S(1)}, bf16[3136,256]{1,0:T(8,128)(2,1)}, u32[]{:S(2)}) copy-start(bf16[3136,256]{1,0:T(8,128)(2,1)} %reshape.71) | copy-start | bytes 4816900
  50.4 1.4 copy-start.12
  51.8 1.4 copy-start.13
  53.2 1.4 copy-start.2
  54.7 1.5 copy-start.1
  76.7 1.4 copy-start.3
  84.5 2.1 copy-start.6
  84.5 2.1 copy-start.7
  86.6 1.5 copy-start.4
  86.6 2.4 copy-start.8
  89.0 1.4 copy-start.9
  90.4 1.4 copy-start.10
  93.2 0.7 copy-start.14
  93.2 1.3 copy-start.15
Sparse Core Ops, SparseCore 0:
  93.3 146.0 all-reduce.4
where the time goes:
time: 260 us; the launch traced here: 257 us
  waiting for transfers between devices  101 us (39%)
  local copies, waits for them, and re-layouts  54.6 us (21%)
  blocking collectives  40.9 us (16%)
  matrix products  30 us (12%)
  other arithmetic  15.6 us (6%)
  between operations  14.2 us (5%)
    psum x1, waiting for transfers between devices, on_device(): lax.psum((mask_local, rpn_local, local_counts), ('gx', 'gy'))  101 us
    psum x1, blocking collectives, on_device(): lax.psum((mask_local, rpn_local, local_counts), ('gx', 'gy'))  40.9 us
    dot_general x18, matrix products, weight_grad(): lax.dot_general(window, flat_cot, (((0,), (0,)), ((), ())), preferred_ele...  30 us
    slice x9, local copies, waits for them, and re-layouts, weight_grad(): padded[:, row_tap:row_tap + grid_rows, col_tap:col_tap + grid_cols, :]  22.6 us
    reshape x8, local copies, waits for them, and re-layouts, weight_grad(): window = padded[:, row_tap:row_tap + grid_rows, col_tap:col_tap + grid_co...  20.2 us
    sub x1, other arithmetic, step_update(): return (weight - 0.02 * fresh_moment, fresh_moment)  10.6 us
    unnamed x34, local copies, waits for them, and re-layouts  5.91 us
  transfers between devices with their start and end apart: 1, of which 1 were waited for; matrix products, arithmetic and copies ran while one was open for 1% of the time, Pallas kernels for 0%

commit v1 on v0

v1 whole, which is shorter than its diff:
```python
import functools

import jax
import jax.numpy as jnp
from jax import lax
from jax.experimental import pallas as pl
from jax.experimental.pallas import tpu as pltpu
from jax.sharding import PartitionSpec as P

MESH = pl.DeviceIdType.MESH
TAPS = 9
LAG = 2


def dot_t(lhs, rhs):
    return lax.dot_general(lhs, rhs, (((0,), (0,)), ((), ())), preferred_element_type=jnp.float32)


def grads_kernel(counts, mask_x, mask_y, rpn_x, rpn_y, mask_g, rpn_g, xs, tmp, ycat_m, ycat_r):
    images, slots, side, _, chans = mask_x.shape
    cols = xs.shape[2]
    roi_rows = cols * cols
    xs[...] = jnp.zeros_like(xs)
    tmp[...] = jnp.zeros_like(tmp)
    ycat_m[...] = jnp.zeros_like(ycat_m)

    def one_roi(i, carry):
        n, s = lax.div(i, slots), lax.rem(i, slots)
        valid = s < counts[n]
        for y in range(side):
            xs[i, y, pl.ds(0, side), :] = mask_x[n, s, y]
            row = mask_y[n, s, y].astype(jnp.float32)
            tmp[y, pl.ds(0, side), :] = jnp.where(valid, row, 0.0)
        v = tmp[...].reshape(side * cols, chans)
        at = pl.ds(pl.multiple_of(cols + i * roi_rows, cols), side * cols)
        ycat_m[at, 0:chans] = pltpu.roll(v, side * cols - 1, 0).astype(jnp.bfloat16)
        ycat_m[at, chans : 2 * chans] = v.astype(jnp.bfloat16)
        ycat_m[at, 2 * chans :] = pltpu.roll(v, 1, 0).astype(jnp.bfloat16)
        return carry

    lax.fori_loop(0, images * slots, one_roi, 0)
    mask_g[...] = jnp.zeros_like(mask_g)
    per = 4
    block = per * roi_rows

    def mask_step(k, carry):
        x = xs[pl.ds(k * per, per)].reshape(block, chans)
        for a in range(3):
            base = pl.multiple_of(k * block + cols - (a - 1) * cols, cols)
            out = dot_t(x, ycat_m[pl.ds(base, block), :])
            for b in range(3):
                mask_g[3 * a + b] += out[:, b * chans : (b + 1) * chans]
        return carry

    lax.fori_loop(0, images * slots // per, mask_step, 0)

    _, grid_rows, grid_cols, _ = rpn_x.shape
    group = 8
    part = group * grid_cols
    rpn_g[...] = jnp.zeros_like(rpn_g)
    where_col = lax.rem(lax.broadcasted_iota(jnp.int32, (part, chans), 0), grid_cols)
    zero_rows = jnp.zeros((grid_cols, 3 * chans), jnp.bfloat16)
    ycat_r[pl.ds(0, grid_cols), :] = zero_rows
    ycat_r[pl.ds((1 + grid_rows) * grid_cols, grid_cols), :] = zero_rows

    def one_image(n, carry):
        def shift(r, inner):
            v = rpn_y[n, pl.ds(r * group, group)].reshape(part, chans)
            wide = v.astype(jnp.float32)
            down = jnp.where(where_col == grid_cols - 1, 0.0, pltpu.roll(wide, part - 1, 0))
            up = jnp.where(where_col == 0, 0.0, pltpu.roll(wide, 1, 0))
            at = pl.ds(pl.multiple_of(grid_cols + r * part, grid_cols), part)
            ycat_r[at, 0:chans] = down.astype(jnp.bfloat16)
            ycat_r[at, chans : 2 * chans] = v
            ycat_r[at, 2 * chans :] = up.astype(jnp.bfloat16)
            return inner

        lax.fori_loop(0, grid_rows // group, shift, 0)
        block_rows = 24
        depth = block_rows * grid_cols

        def rpn_step(k, inner):
            x = rpn_x[n, pl.ds(k * block_rows, block_rows)].reshape(depth, chans)
            for a in range(3):
                base = pl.multiple_of(k * depth + grid_cols - (a - 1) * grid_cols, grid_cols)
                out = dot_t(x, ycat_r[pl.ds(base, depth), :])
                for b in range(3):
                    rpn_g[3 * a + b] += out[:, b * chans : (b + 1) * chans]
            return inner

        lax.fori_loop(0, grid_rows // block_rows, rpn_step, 0)
        return carry

    lax.fori_loop(0, images, one_image, 0)


def local_grads(roi_counts, mask_feats, mask_cot, rpn_feats, rpn_cot):
    images, slots, side, _, chans = mask_feats.shape
    _, grid_rows, grid_cols, _ = rpn_feats.shape
    cols = -(-(side + 1) // 16) * 16
    vmem = pl.BlockSpec(memory_space=pltpu.VMEM)
    rows_m = images * slots * cols * cols
    out = jax.ShapeDtypeStruct((TAPS, chans, chans), jnp.float32)
    return pl.pallas_call(
        grads_kernel,
        out_shape=(out, out),
        in_specs=[pl.BlockSpec(memory_space=pltpu.SMEM)] + [vmem] * 4,
        out_specs=(vmem, vmem),
        scratch_shapes=[
            pltpu.VMEM((images * slots, cols, cols, chans), jnp.bfloat16),
            pltpu.VMEM((side, cols, chans), jnp.float32),
            pltpu.VMEM((rows_m + 2 * cols, 3 * chans), jnp.bfloat16),
            pltpu.VMEM(((grid_rows + 2) * grid_cols, 3 * chans), jnp.bfloat16),
        ],
        compiler_params=pltpu.CompilerParams(vmem_limit_bytes=56 * 2**20),
        name="grads",
    )(roi_counts, mask_feats, mask_cot, rpn_feats, rpn_cot)


def splits(rows, size):
    return rows % (8 * size) == 0


def groups_here(n_gx, n_gy):
    gx, gy = lax.axis_index("gx"), lax.axis_index("gy")
    core, x = lax.rem(gx, 2), lax.div(gx, 2)
    y, z = lax.rem(gy, 2), lax.div(gy, 2)
    core_group = (2, core, lambda m: (x * 2 + m, gy))
    x_group = (n_gx // 2, x, lambda m: (m * 2 + core, gy))
    y_group = (2, y, lambda m: (gx, z * 2 + m))
    z_group = (n_gy // 2, z, lambda m: (gx, m * 2 + y))
    return core_group, x_group, y_group, z_group


def members(group):
    size, own, device = group
    return [
        (k, lax.rem(own + 1 + k, size), size - 2 - k, device) for k in range(size - 1)
    ]


def sum_kernel(n_gx, n_gy, *refs):
    roi, anchor, mask_g, rpn_g, mask_mo, rpn_mo, mask_out, rpn_out = refs[:8]
    acc, mine, mine_sem, cnt, cnt_in = refs[8:13]
    landing = (refs[13:17], refs[17:21])
    cnt_sems = refs[21:25]
    cnt_send = refs[25:29]
    rs_recv = (refs[29:33], refs[33:37])
    rs_send = (refs[37:41], refs[41:45])
    ag_recv = (refs[45:49], refs[49:53])
    ag_send = (refs[53:57], refs[57:61])
    core_g, x_g, y_g, z_g = groups_here(n_gx, n_gy)
    orders = ((core_g, x_g, y_g, z_g), (core_g, y_g, x_g, z_g))
    grads, outs, moments = (mask_g, rpn_g), (mask_out, rpn_out), (mask_mo, rpn_mo)
    chunk = mask_g.shape[1]
    chunks = mask_g.shape[0]

    blocks, offs = [], []
    cut = ([], [])
    for color in range(2):
        b, o, bs, os = chunk, 0, [], [0]
        rest = chunk
        for size, _, _ in orders[color]:
            cut[color].append(splits(rest, size))
            rest = rest // size if cut[color][-1] else rest
        for size, own, _ in orders[color]:
            if splits(b, size):
                b = b // size
                o = o + own * b
            bs.append(b)
            os.append(o)
        blocks.append(bs)
        offs.append(os)
    piece = blocks[0][3]

    barrier = pltpu.get_barrier_semaphore()
    total = 0
    for g in orders[0]:
        for _, m, _, device in members(g):
            pl.semaphore_signal(barrier, inc=1, device_id=device(m), device_id_type=MESH)
            total += 1

    def own_rows(color, j):
        return pltpu.make_async_copy(
            moments[color].at[j, pl.ds(pl.multiple_of(offs[color][4], 8), piece), :],
            mine.at[color, j],
            mine_sem.at[color, j],
        )

    def start_moments(j, carry):
        own_rows(0, j).start()
        own_rows(1, j).start()
        return carry

    lax.fori_loop(0, chunks, start_moments, 0)
    half = cnt.shape[1] // 2
    lanes = cnt.shape[2]
    for which, ref in ((0, roi), (1, anchor)):
        s = ref[0]
        for i in range(1, ref.shape[0]):
            s = s + ref[i]
        cnt[0, which * half : (which + 1) * half, :] = jnp.full(
            (half, lanes), s.astype(jnp.float32), jnp.float32
        )
    pl.semaphore_wait(barrier, total)

    def cnt_copy(s, k, m, far, device):
        return pltpu.make_async_remote_copy(
            src_ref=cnt.at[s],
            dst_ref=cnt_in.at[s, far],
            send_sem=cnt_send[s].at[k],
            recv_sem=cnt_sems[s].at[far],
            device_id=device(m),
            device_id_type=MESH,
        )

    def cnt_arrival(s, k, m, device):
        return pltpu.make_async_remote_copy(
            src_ref=cnt.at[s],
            dst_ref=cnt_in.at[s, k],
            send_sem=cnt_send[s].at[k],
            recv_sem=cnt_sems[s].at[k],
            device_id=device(m),
            device_id_type=MESH,
        )

    def cnt_start(s):
        for k, m, far, device in members(orders[0][s]):
            cnt_copy(s, k, m, far, device).start()

    def cnt_finish(s):
        value = cnt[s]
        for k, m, far, device in members(orders[0][s]):
            cnt_arrival(s, k, m, device).wait_recv()
            value = value + cnt_in[s, k]
        cnt[s + 1] = value

    def rs_copy(color, s, j, k, m, far, device):
        b = blocks[color][s]
        start = offs[color][s] + (m * b if cut[color][s] else 0)
        rows = pl.ds(pl.multiple_of(start, 8), b)
        source = grads[color].at[j, rows, :] if s == 0 else acc.at[color, j, rows, :]
        return pltpu.make_async_remote_copy(
            src_ref=source,
            dst_ref=landing[color][s].at[j, far],
            send_sem=rs_send[color][s].at[j, k],
            recv_sem=rs_recv[color][s].at[j, far],
            device_id=device(m),
            device_id_type=MESH,
        )

    def rs_arrival(color, s, j, k, m, device):
        b = blocks[color][s]
        start = offs[color][s] + (m * b if cut[color][s] else 0)
        rows = pl.ds(pl.multiple_of(start, 8), b)
        source = grads[color].at[j, rows, :] if s == 0 else acc.at[color, j, rows, :]
        return pltpu.make_async_remote_copy(
            src_ref=source,
            dst_ref=landing[color][s].at[j, k],
            send_sem=rs_send[color][s].at[j, k],
            recv_sem=rs_recv[color][s].at[j, k],
            device_id=device(m),
            device_id_type=MESH,
        )

    def rs_start(color, s, j):
        for k, m, far, device in members(orders[color][s]):
            rs_copy(color, s, j, k, m, far, device).start()

    def rs_sum(color, s, j):
        b = blocks[color][s]
        rows = pl.ds(pl.multiple_of(offs[color][s + 1], 8), b)
        value = grads[color][j, rows, :] if s == 0 else acc[color, j, rows, :]
        for k, m, _, device in members(orders[color][s]):
            rs_arrival(color, s, j, k, m, device).wait_recv()
            if cut[color][s]:
                value = value + landing[color][s][j, k]
        if not cut[color][s]:
            size, own, _ = orders[color][s]
            terms = []
            for m in range(size):
                slot = lax.rem(m - own - 1 + 2 * size, size)
                slot = jnp.minimum(slot, max(size - 2, 0))
                here = own == m
                terms.append(jnp.where(here, value, landing[color][s][j, slot]))
            value = functools.reduce(jnp.add, terms) if size > 1 else value
        if s < 3:
            acc[color, j, rows, :] = value
        else:
            own_rows(color, j).wait()
            count = cnt[4, color * half : (color + 1) * half, :][0:1, :]
            count = jnp.concatenate([count] * (value.shape[1] // lanes), axis=1)
            outs[color][j, rows, :] = 0.9 * mine[color, j] + value / count

    def ag_copy(color, s, j, k, m, far, device):
        b = blocks[color][s]
        rows = pl.ds(pl.multiple_of(offs[color][s + 1], 8), b)
        return pltpu.make_async_remote_copy(
            src_ref=outs[color].at[j, rows, :],
            dst_ref=outs[color].at[j, rows, :],
            send_sem=ag_send[color][s].at[j, k],
            recv_sem=ag_recv[color][s].at[j, far],
            device_id=device(m),
            device_id_type=MESH,
        )

    def ag_arrival(color, s, j, k, m, device):
        b = blocks[color][s]
        rows = pl.ds(pl.multiple_of(offs[color][s] + m * b, 8), b)
        return pltpu.make_async_remote_copy(
            src_ref=outs[color].at[j, rows, :],
            dst_ref=outs[color].at[j, rows, :],
            send_sem=ag_send[color][s].at[j, k],
            recv_sem=ag_recv[color][s].at[j, k],
            device_id=device(m),
            device_id_type=MESH,
        )

    def ag_start(color, s, j):
        if not cut[color][s]:
            return
        for k, m, far, device in members(orders[color][s]):
            ag_copy(color, s, j, k, m, far, device).start()

    def ag_wait(color, s, j):
        if not cut[color][s]:
            return
        for k, m, _, device in members(orders[color][s]):
            ag_arrival(color, s, j, k, m, device).wait_recv()

    def at_stage(t, lag, work):
        j = t - lag

        @pl.when((j >= 0) & (j < chunks))
        def _():
            work(j)

    def tick(t, carry):
        def first(j):
            for color in range(2):
                rs_start(color, 0, j)

        at_stage(t, 0, first)
        for s in range(4):

            @pl.when(t == LAG * (s + 1))
            def _(s=s):
                cnt_finish(s)
                if s < 3:
                    cnt_start(s + 1)

        for s in range(4):

            def reduce(j, s=s):
                for color in range(2):
                    rs_sum(color, s, j)
                for color in range(2):
                    if s < 3:
                        rs_start(color, s + 1, j)
                    else:
                        ag_start(color, 3, j)

            at_stage(t, LAG * (s + 1), reduce)
        for s in (3, 2, 1, 0):

            def gather(j, s=s):
                for color in range(2):
                    ag_wait(color, s, j)
                    if s > 0:
                        ag_start(color, s - 1, j)

            at_stage(t, LAG * (8 - s), gather)
        return carry

    cnt_start(0)
    lax.fori_loop(0, chunks + 8 * LAG, tick, 0)

    def drain(j, carry):
        for color in range(2):
            for s in range(4):
                for k, m, far, device in members(orders[color][s]):
                    rs_copy(color, s, j, k, m, far, device).wait_send()
                    if cut[color][s]:
                        ag_copy(color, s, j, k, m, far, device).wait_send()
        return carry

    lax.fori_loop(0, chunks, drain, 0)
    for s in range(4):
        for k, m, far, device in members(orders[0][s]):
            cnt_copy(s, k, m, far, device).wait_send()


def summed_moments(n_gx, n_gy, roi_counts, anchor_counts, mask_g, rpn_g, mask_mo, rpn_mo):
    chunks, chunk, chans = mask_g.shape
    sizes = ((2, n_gx // 2, 2, n_gy // 2), (2, 2, n_gx // 2, n_gy // 2))
    smem, vmem = pl.BlockSpec(memory_space=pltpu.SMEM), pl.BlockSpec(memory_space=pltpu.VMEM)
    hbm = pl.BlockSpec(memory_space=pl.ANY)
    widest = max(max(s) for s in sizes) - 1
    landing, sems = [], []
    for color in range(2):
        b = chunk
        for size in sizes[color]:
            b = b // size if splits(b, size) else b
            landing.append(pltpu.VMEM((chunks, max(size - 1, 1), b, chans), jnp.float32))
            sems.append(pltpu.SemaphoreType.DMA((chunks, max(size - 1, 1))))
    piece = b
    small = [pltpu.SemaphoreType.DMA((max(size - 1, 1),)) for size in sizes[0]]
    out = jax.ShapeDtypeStruct(mask_g.shape, jnp.float32)
    return pl.pallas_call(
        functools.partial(sum_kernel, n_gx, n_gy),
        out_shape=(out, out),
        in_specs=[smem, smem, vmem, vmem, hbm, hbm],
        out_specs=(vmem, vmem),
        scratch_shapes=[
            pltpu.VMEM((2, chunks, chunk, chans), jnp.float32),
            pltpu.VMEM((2, chunks, piece, chans), jnp.float32),
            pltpu.SemaphoreType.DMA((2, chunks)),
            pltpu.VMEM((5, 16, 128), jnp.float32),
            pltpu.VMEM((4, widest, 16, 128), jnp.float32),
        ]
        + landing
        + small
        + small
        + sems * 4,
        compiler_params=pltpu.CompilerParams(
            collective_id=0, has_side_effects=True, vmem_limit_bytes=40 * 2**20
        ),
        name="sum_and_share",
    )(roi_counts, anchor_counts, mask_g, rpn_g, mask_mo, rpn_mo)


def on_device(
    n_gx,
    n_gy,
    mask_feats,
    mask_cot,
    roi_counts,
    rpn_feats,
    rpn_cot,
    anchor_counts,
    mask_weight,
    rpn_weight,
    mask_moment,
    rpn_moment,
):
    mask_g, rpn_g = local_grads(roi_counts, mask_feats, mask_cot, rpn_feats, rpn_cot)
    new_mask, new_rpn = summed_moments(
        n_gx,
        n_gy,
        roi_counts,
        anchor_counts,
        mask_g,
        rpn_g,
        mask_moment.reshape(mask_g.shape),
        rpn_moment.reshape(rpn_g.shape),
    )
    new_mask, new_rpn = new_mask.reshape(mask_moment.shape), new_rpn.reshape(rpn_moment.shape)
    return (mask_weight - 0.02 * new_mask, rpn_weight - 0.02 * new_rpn, new_mask, new_rpn)


def solution(mesh):
    split = P(("gx", "gy"))
    placed = (split,) * 6 + (P(),) * 4
    return jax.shard_map(
        functools.partial(on_device, mesh.shape["gx"], mesh.shape["gy"]),
        mesh=mesh,
        in_specs=placed,
        out_specs=(P(), P(), P(), P()),
        check_vma=False,
    )
```

time: 260 us -> 90.4 us (0.35); the launches traced: 257 us -> 90.2 us
  waiting for transfers between devices: 101 us -> 0 us
  Pallas kernels: 0 us -> 75.7 us
  local copies, waits for them, and re-layouts: 54.6 us -> 11 us
  blocking collectives: 40.9 us -> 0 us
  matrix products: 30 us -> 0 us
  between operations: 14.2 us -> 0.69 us
  other arithmetic: 15.6 us -> 2.82 us
    psum x1 -> x0, waiting for transfers between devices: 101 us -> none  [on_device(): lax.psum((mask_local, rpn_local, local_counts), ('gx', 'gy'))]
    pallas_call x0 -> x2, Pallas kernels: none -> 75.7 us  [the longest x1 56.8 us: summed_moments(): pl.pallas_call(functools.partial(sum_kernel, n_gx, n_gy), out_shape=(out,...]
    psum x1 -> x0, blocking collectives: 40.9 us -> none  [on_device(): lax.psum((mask_local, rpn_local, local_counts), ('gx', 'gy'))]
    dot_general x18 -> x0, matrix products: 30 us -> none  [weight_grad(): lax.dot_general(window, flat_cot, (((0,), (0,)), ((), ())), preferred_ele...]
    slice x10 -> x0, local copies, waits for them, and re-layouts: 23.3 us -> none  [the longest x9 22.6 us: weight_grad(): padded[:, row_tap:row_tap + grid_rows, col_tap:col_tap + grid_cols, :]]
    reshape x8 -> x0, local copies, waits for them, and re-layouts: 20.2 us -> none  [weight_grad(): window = padded[:, row_tap:row_tap + grid_rows, col_tap:col_tap + grid_co...]
    sub x1, other arithmetic: 10.6 us -> 2.82 us  [on_device(): rpn_weight - 0.02 * new_rpn]
    unnamed x34 -> x22, local copies, waits for them, and re-layouts: 5.91 us -> 11 us
  transfers between devices with their start and end apart: 1 -> 0, of which waited for: 1 -> 0; matrix products, arithmetic and copies ran while one was open for 1% -> 0% of each run, Pallas kernels for 0% -> 0%
where the time goes in v1:
time: 90.4 us; the launch traced here: 90.2 us
  Pallas kernels  75.7 us (84%)
  local copies, waits for them, and re-layouts  11 us (12%)
  other arithmetic  2.82 us (3%)
    pallas_call x1, Pallas kernels, summed_moments(): pl.pallas_call(functools.partial(sum_kernel, n_gx, n_gy), out_shape=(out,...  56.8 us
    pallas_call x1, Pallas kernels, local_grads(): pl.pallas_call(grads_kernel, out_shape=(out, out), in_specs=[pl.BlockSpec...  18.9 us
    unnamed x22, local copies, waits for them, and re-layouts  11 us
    sub x1, other arithmetic, on_device(): rpn_weight - 0.02 * new_rpn  2.82 us

profile of v1, /device:TPU:1, one launch (start us, length us, event | category | flops | bytes accessed | tf_op | source)
XLA Modules:
  0.0 90.2 jit_solution(6114633521753244535)
XLA Ops:
  0.6 0.0 copy-start.8
  0.6 3.2 %copy.14.mask_x = bf16[2,8,14,14,256]{4,3,2,1,0:T(8,128)(2,1)} copy(bf16[2,8,14,14,256]{4,1,3,2,0:T(8,128)(2,1)} %param.10) | data formatting | bytes 3211264 | tf_op args[0]
  3.8 0.0 copy-done.8
  3.8 1.6 %copy.15.mask_y = bf16[2,8,14,14,256]{4,3,2,1,0:T(8,128)(2,1)} copy(bf16[2,8,14,14,256]{4,1,3,2,0:T(8,128)(2,1)S(1)} %copy-done.8) | data formatting | bytes 3211264 | tf_op args[1]
  5.5 0.0 copy-start
  5.5 0.0 copy-start.1
  5.5 0.0 copy-start.4
  5.5 0.0 copy-start.5
  5.5 18.9 %grads.1 = (f32[9,256,256]{2,1,0:T(8,128)}, f32[9,256,256]{2,1,0:T(8,128)}) custom-call(s32[2]{0:T(128)} %refs_0_.1, bf16[2,8,14,14,256]{4,3,2,1,0:T(8,128)(2,1)} %copy.14.mask_x, bf16[2,8,14,14,256]{4,3,2,1,0:T(8,128)(2,1)} %copy.15.mask_y, bf16[2,48,32,256]{3,2,1,0:T(8,128)(2,1)} %rpn_x.1, bf16[2,48,32,256]{3,2,1,0:T(8,128)(2,1)} %rpn_y.1), custom_call_target="tpu_custom_call" | custom-call | tf_op jit(solution)/shard_map/grads/pallas_call | solution.py:104
  24.4 0.0 copy-done
  24.4 0.0 copy-done.1
  24.4 0.0 copy-done.4
  24.4 0.0 copy-done.5
  24.4 0.0 copy-start.2
  24.4 1.7 %copy-done.2 = f32[9,256,256]{2,1,0:T(8,128)S(1)} copy-done((f32[9,256,256]{2,1,0:T(8,128)S(1)}, f32[9,256,256]{2,1,0:T(8,128)}, u32[]{:S(2)}) %copy-start.2) | copy-done | bytes 2359320
  26.1 0.0 copy-start.3
  26.1 1.7 %copy-done.3 = f32[9,256,256]{2,1,0:T(8,128)S(1)} copy-done((f32[9,256,256]{2,1,0:T(8,128)S(1)}, f32[9,256,256]{2,1,0:T(8,128)}, u32[]{:S(2)}) %copy-start.3) | copy-done | bytes 2359320
  27.8 0.0 copy-start.6
  27.8 0.0 copy-start.7
  27.8 56.8 %sum_and_share.1 = (f32[9,256,256]{2,1,0:T(8,128)S(1)}, f32[9,256,256]{2,1,0:T(8,128)S(1)}) custom-call(s32[2]{0:T(128)S(1)} %copy-done.4, s32[2]{0:T(128)S(1)} %copy-done.5, f32[9,256,256]{2,1,0:T(8,128)S(1)} %copy-done.2, f32[9,256,256]{2,1,0:T(8,128)S(1)} %copy-done.3, f32[9,256,256]{2,1,0:T(8,128)S(1)} %bitcast.8, f32[9,256,256]{2,1,0:T(8,128)S(1)} %bitcast.9), custom_call_target="tpu_custom_call" | custom-call | tf_op jit(solution)/shard_map/sum_and_share/pallas_call | solution.py:409
  84.6 0.0 copy-done.6
  84.6 0.0 copy-done.7
  84.6 2.8 %multiply_subtract_fusion = (f32[2304,256]{1,0:T(8,128)}, f32[2304,256]{1,0:T(8,128)}) fusion(f32[2304,256]{1,0:T(8,128)S(1)} %copy-done.6, f32[2304,256]{1,0:T(8,128)S(1)} %copy-done.7, f32[9,256,256]{2,1,0:T(8,128)S(1)} %get-tuple-element.10, f32[9,256,256]{2,1,0:T(8,128)S(1)} %get-tuple-element.11), kind=kLoop, calls=%fused_computation | loop fusion | flops 2359296 | bytes 14155776 | tf_op jit(solution)/shard_map/sub | solution.py:458
  87.4 1.4 %copy.18 = f32[2304,256]{1,0:T(8,128)} copy(f32[2304,256]{1,0:T(8,128)S(1)} %bitcast.7) | data formatting | bytes 4718592
  88.8 1.4 %copy.19 = f32[2304,256]{1,0:T(8,128)} copy(f32[2304,256]{1,0:T(8,128)S(1)} %bitcast.6) | data formatting | bytes 4718592
Async XLA Ops:
  0.6 3.2 %copy-start.8 = (bf16[2,8,14,14,256]{4,1,3,2,0:T(8,128)(2,1)S(1)}, bf16[2,8,14,14,256]{4,1,3,2,0:T(8,128)(2,1)}, u32[]{:S(2)}) copy-start(bf16[2,8,14,14,256]{4,1,3,2,0:T(8,128)(2,1)} %param.11) | copy-start | bytes 4816900
  5.5 19.0 %copy-start = (f32[2304,256]{1,0:T(8,128)S(1)}, f32[2304,256]{1,0:T(8,128)}, u32[]{:S(2)}) copy-start(f32[2304,256]{1,0:T(8,128)} %param.18) | copy-start | bytes 7077892
  5.5 19.0 %copy-start.1 = (f32[2304,256]{1,0:T(8,128)S(1)}, f32[2304,256]{1,0:T(8,128)}, u32[]{:S(2)}) copy-start(f32[2304,256]{1,0:T(8,128)} %param.19) | copy-start | bytes 7077892
  5.5 19.0 %copy-start.4 = (s32[2]{0:T(128)S(1)}, s32[2]{0:T(128)}, u32[]{:S(2)}) copy-start(s32[2]{0:T(128)} %refs_0_.1) | copy-start | bytes 28
  5.5 19.0 %copy-start.5 = (s32[2]{0:T(128)S(1)}, s32[2]{0:T(128)}, u32[]{:S(2)}) copy-start(s32[2]{0:T(128)} %refs_1_.1) | copy-start | bytes 28
  24.4 1.7 %copy-start.2 = (f32[9,256,256]{2,1,0:T(8,128)S(1)}, f32[9,256,256]{2,1,0:T(8,128)}, u32[]{:S(2)}) copy-start(f32[9,256,256]{2,1,0:T(8,128)} %get-tuple-element.8.refs_2_) | copy-start | bytes 7077892
  26.1 1.7 %copy-start.3 = (f32[9,256,256]{2,1,0:T(8,128)S(1)}, f32[9,256,256]{2,1,0:T(8,128)}, u32[]{:S(2)}) copy-start(f32[9,256,256]{2,1,0:T(8,128)} %get-tuple-element.9.refs_3_) | copy-start | bytes 7077892
  27.8 56.8 %copy-start.6 = (f32[2304,256]{1,0:T(8,128)S(1)}, f32[2304,256]{1,0:T(8,128)}, u32[]{:S(2)}) copy-start(f32[2304,256]{1,0:T(8,128)} %param.17) | copy-start | bytes 7077892
  27.8 56.8 %copy-start.7 = (f32[2304,256]{1,0:T(8,128)S(1)}, f32[2304,256]{1,0:T(8,128)}, u32[]{:S(2)}) copy-start(f32[2304,256]{1,0:T(8,128)} %param.16) | copy-start | bytes 7077892

commit v2 on v1

--- a/solution.py
+++ b/solution.py
@@ -9,112 +9,61 @@
 
 MESH = pl.DeviceIdType.MESH
 TAPS = 9
-LAG = 2
-
-
-def dot_t(lhs, rhs):
-    return lax.dot_general(lhs, rhs, (((0,), (0,)), ((), ())), preferred_element_type=jnp.float32)
-
-
-def grads_kernel(counts, mask_x, mask_y, rpn_x, rpn_y, mask_g, rpn_g, xs, tmp, ycat_m, ycat_r):
-    images, slots, side, _, chans = mask_x.shape
-    cols = xs.shape[2]
-    roi_rows = cols * cols
-    xs[...] = jnp.zeros_like(xs)
-    tmp[...] = jnp.zeros_like(tmp)
-    ycat_m[...] = jnp.zeros_like(ycat_m)
-
-    def one_roi(i, carry):
-        n, s = lax.div(i, slots), lax.rem(i, slots)
-        valid = s < counts[n]
-        for y in range(side):
-            xs[i, y, pl.ds(0, side), :] = mask_x[n, s, y]
-            row = mask_y[n, s, y].astype(jnp.float32)
-            tmp[y, pl.ds(0, side), :] = jnp.where(valid, row, 0.0)
-        v = tmp[...].reshape(side * cols, chans)
-        at = pl.ds(pl.multiple_of(cols + i * roi_rows, cols), side * cols)
-        ycat_m[at, 0:chans] = pltpu.roll(v, side * cols - 1, 0).astype(jnp.bfloat16)
-        ycat_m[at, chans : 2 * chans] = v.astype(jnp.bfloat16)
-        ycat_m[at, 2 * chans :] = pltpu.roll(v, 1, 0).astype(jnp.bfloat16)
-        return carry
-
-    lax.fori_loop(0, images * slots, one_roi, 0)
-    mask_g[...] = jnp.zeros_like(mask_g)
-    per = 4
-    block = per * roi_rows
-
-    def mask_step(k, carry):
-        x = xs[pl.ds(k * per, per)].reshape(block, chans)
-        for a in range(3):
-            base = pl.multiple_of(k * block + cols - (a - 1) * cols, cols)
-            out = dot_t(x, ycat_m[pl.ds(base, block), :])
-            for b in range(3):
-                mask_g[3 * a + b] += out[:, b * chans : (b + 1) * chans]
-        return carry
-
-    lax.fori_loop(0, images * slots // per, mask_step, 0)
-
-    _, grid_rows, grid_cols, _ = rpn_x.shape
-    group = 8
-    part = group * grid_cols
-    rpn_g[...] = jnp.zeros_like(rpn_g)
-    where_col = lax.rem(lax.broadcasted_iota(jnp.int32, (part, chans), 0), grid_cols)
-    zero_rows = jnp.zeros((grid_cols, 3 * chans), jnp.bfloat16)
-    ycat_r[pl.ds(0, grid_cols), :] = zero_rows
-    ycat_r[pl.ds((1 + grid_rows) * grid_cols, grid_cols), :] = zero_rows
-
-    def one_image(n, carry):
-        def shift(r, inner):
-            v = rpn_y[n, pl.ds(r * group, group)].reshape(part, chans)
-            wide = v.astype(jnp.float32)
-            down = jnp.where(where_col == grid_cols - 1, 0.0, pltpu.roll(wide, part - 1, 0))
-            up = jnp.where(where_col == 0, 0.0, pltpu.roll(wide, 1, 0))
-            at = pl.ds(pl.multiple_of(grid_cols + r * part, grid_cols), part)
-            ycat_r[at, 0:chans] = down.astype(jnp.bfloat16)
-            ycat_r[at, chans : 2 * chans] = v
-            ycat_r[at, 2 * chans :] = up.astype(jnp.bfloat16)
-            return inner
-
-        lax.fori_loop(0, grid_rows // group, shift, 0)
-        block_rows = 24
-        depth = block_rows * grid_cols
-
-        def rpn_step(k, inner):
-            x = rpn_x[n, pl.ds(k * block_rows, block_rows)].reshape(depth, chans)
-            for a in range(3):
-                base = pl.multiple_of(k * depth + grid_cols - (a - 1) * grid_cols, grid_cols)
-                out = dot_t(x, ycat_r[pl.ds(base, depth), :])
-                for b in range(3):
-                    rpn_g[3 * a + b] += out[:, b * chans : (b + 1) * chans]
-            return inner
-
-        lax.fori_loop(0, grid_rows // block_rows, rpn_step, 0)
-        return carry
-
-    lax.fori_loop(0, images, one_image, 0)
-
-
-def local_grads(roi_counts, mask_feats, mask_cot, rpn_feats, rpn_cot):
-    images, slots, side, _, chans = mask_feats.shape
-    _, grid_rows, grid_cols, _ = rpn_feats.shape
-    cols = -(-(side + 1) // 16) * 16
-    vmem = pl.BlockSpec(memory_space=pltpu.VMEM)
-    rows_m = images * slots * cols * cols
-    out = jax.ShapeDtypeStruct((TAPS, chans, chans), jnp.float32)
-    return pl.pallas_call(
-        grads_kernel,
-        out_shape=(out, out),
-        in_specs=[pl.BlockSpec(memory_space=pltpu.SMEM)] + [vmem] * 4,
-        out_specs=(vmem, vmem),
-        scratch_shapes=[
-            pltpu.VMEM((images * slots, cols, cols, chans), jnp.bfloat16),
-            pltpu.VMEM((side, cols, chans), jnp.float32),
-            pltpu.VMEM((rows_m + 2 * cols, 3 * chans), jnp.bfloat16),
-            pltpu.VMEM(((grid_rows + 2) * grid_cols, 3 * chans), jnp.bfloat16),
-        ],
-        compiler_params=pltpu.CompilerParams(vmem_limit_bytes=56 * 2**20),
-        name="grads",
-    )(roi_counts, mask_feats, mask_cot, rpn_feats, rpn_cot)
+LAGS = (1, 2, 2, 2, 2, 2, 2, 1)
+DUE = tuple(sum(LAGS[: s + 1]) for s in range(8))
+
+
+def lay_out(x, y, xt, ycat, width, step, count):
+    images, depth, chans = x.shape
+    lanes = 128
+    part = width * max(256 // width, 1)
+    while depth % part:
+        part -= width
+    row = lax.broadcasted_iota(jnp.int32, (part, chans), 0)
+    col = lax.rem(row, width)
+    for n in range(images):
+        for b in range(3):
+            ycat[b, n, pl.ds(0, width), :] = jnp.zeros((width, chans), jnp.bfloat16)
+            tail = ycat.shape[2] - width - depth
+            ycat[b, n, pl.ds(width + depth, tail), :] = jnp.zeros((tail, chans), jnp.bfloat16)
+        live = None if count is None else lax.rem(row, step) < count[n]
+
+        def turn(k, carry, n=n):
+            at = pl.ds(pl.multiple_of(k * lanes, lanes), lanes)
+            xt[n, :, at] = x[n, at, :].T
+            return carry
+
+        lax.fori_loop(0, depth // lanes, turn, 0)
+        rest = depth % lanes
+        if rest:
+            last = x[n, pl.ds(depth - rest, rest), :]
+            fill = jnp.zeros((lanes - rest, chans), last.dtype)
+            xt[n, :, pl.ds(depth - rest, lanes)] = jnp.concatenate([last, fill], axis=0).T
+
+        def move(k, carry, n=n, live=live):
+            v = y[n, pl.ds(pl.multiple_of(k * part, 16), part), :].astype(jnp.float32)
+            if live is not None:
+                v = jnp.where(live, v, 0.0)
+            down = jnp.where(col >= width - step, 0.0, pltpu.roll(v, part - step, 0))
+            up = jnp.where(col < step, 0.0, pltpu.roll(v, step, 0))
+            at = pl.ds(pl.multiple_of(width + k * part, 16), part)
+            ycat[0, n, at, :] = down.astype(jnp.bfloat16)
+            ycat[1, n, at, :] = v.astype(jnp.bfloat16)
+            ycat[2, n, at, :] = up.astype(jnp.bfloat16)
+            return carry
+
+        lax.fori_loop(0, depth // part, move, 0)
+
+
+def one_tap(j, xt, ycat, grad, width):
+    images, _, depth = xt.shape
+    a, b = lax.div(j, 3), lax.rem(j, 3)
+    at = pl.ds(pl.multiple_of((2 - a) * width, 16), depth)
+    total = None
+    for n in range(images):
+        term = jnp.dot(xt[n], ycat[b, n, at, :], preferred_element_type=jnp.float32)
+        total = term if total is None else total + term
+    grad[j] = total
 
 
 def splits(rows, size):
@@ -139,9 +88,12 @@
     ]
 
 
-def sum_kernel(n_gx, n_gy, *refs):
-    roi, anchor, mask_g, rpn_g, mask_mo, rpn_mo, mask_out, rpn_out = refs[:8]
-    acc, mine, mine_sem, cnt, cnt_in = refs[8:13]
+def sum_kernel(n_gx, n_gy, widths, steps, *refs):
+    roi, anchor = refs[:2]
+    given, moments, outs = refs[2:6], refs[6:8], refs[8:10]
+    mine, mine_sem, cnt, cnt_in = refs[10:14]
+    xts, ycats, grads = refs[14:16], refs[16:18], refs[18:20]
+    refs = refs[7:]
     landing = (refs[13:17], refs[17:21])
     cnt_sems = refs[21:25]
     cnt_send = refs[25:29]
@@ -151,9 +103,7 @@
     ag_send = (refs[53:57], refs[57:61])
     core_g, x_g, y_g, z_g = groups_here(n_gx, n_gy)
     orders = ((core_g, x_g, y_g, z_g), (core_g, y_g, x_g, z_g))
-    grads, outs, moments = (mask_g, rpn_g), (mask_out, rpn_out), (mask_mo, rpn_mo)
-    chunk = mask_g.shape[1]
-    chunks = mask_g.shape[0]
+    chunks, chunk = grads[0].shape[:2]
 
     blocks, offs = [], []
     cut = ([], [])
@@ -202,6 +152,16 @@
         cnt[0, which * half : (which + 1) * half, :] = jnp.full(
             (half, lanes), s.astype(jnp.float32), jnp.float32
         )
+    for color, count in ((0, roi), (1, None)):
+        lay_out(
+            given[2 * color],
+            given[2 * color + 1],
+            xts[color],
+            ycats[color],
+            widths[color],
+            steps[color],
+            count,
+        )
     pl.semaphore_wait(barrier, total)
 
     def cnt_copy(s, k, m, far, device):
@@ -239,7 +199,7 @@
         b = blocks[color][s]
         start = offs[color][s] + (m * b if cut[color][s] else 0)
         rows = pl.ds(pl.multiple_of(start, 8), b)
-        source = grads[color].at[j, rows, :] if s == 0 else acc.at[color, j, rows, :]
+        source = grads[color].at[j, rows, :]
         return pltpu.make_async_remote_copy(
             src_ref=source,
             dst_ref=landing[color][s].at[j, far],
@@ -253,7 +213,7 @@
         b = blocks[color][s]
         start = offs[color][s] + (m * b if cut[color][s] else 0)
         rows = pl.ds(pl.multiple_of(start, 8), b)
-        source = grads[color].at[j, rows, :] if s == 0 else acc.at[color, j, rows, :]
+        source = grads[color].at[j, rows, :]
         return pltpu.make_async_remote_copy(
             src_ref=source,
             dst_ref=landing[color][s].at[j, k],
@@ -270,7 +230,7 @@
     def rs_sum(color, s, j):
         b = blocks[color][s]
         rows = pl.ds(pl.multiple_of(offs[color][s + 1], 8), b)
-        value = grads[color][j, rows, :] if s == 0 else acc[color, j, rows, :]
+        value = grads[color][j, rows, :]
         for k, m, _, device in members(orders[color][s]):
             rs_arrival(color, s, j, k, m, device).wait_recv()
             if cut[color][s]:
@@ -285,7 +245,7 @@
                 terms.append(jnp.where(here, value, landing[color][s][j, slot]))
             value = functools.reduce(jnp.add, terms) if size > 1 else value
         if s < 3:
-            acc[color, j, rows, :] = value
+            grads[color][j, rows, :] = value
         else:
             own_rows(color, j).wait()
             count = cnt[4, color * half : (color + 1) * half, :][0:1, :]
@@ -340,15 +300,25 @@
             for color in range(2):
                 rs_start(color, 0, j)
 
-        at_stage(t, 0, first)
+        at_stage(t, 1, first)
+
         for s in range(4):
 
-            @pl.when(t == LAG * (s + 1))
+            @pl.when(t == DUE[s])
             def _(s=s):
                 cnt_finish(s)
                 if s < 3:
                     cnt_start(s + 1)
 
+        for s in (3, 2, 1, 0):
+
+            def gather(j, s=s):
+                for color in range(2):
+                    ag_wait(color, s, j)
+                    if s > 0:
+                        ag_start(color, s - 1, j)
+
+            at_stage(t, 1 + DUE[7 - s], gather)
         for s in range(4):
 
             def reduce(j, s=s):
@@ -360,20 +330,17 @@
                     else:
                         ag_start(color, 3, j)
 
-            at_stage(t, LAG * (s + 1), reduce)
-        for s in (3, 2, 1, 0):
-
-            def gather(j, s=s):
-                for color in range(2):
-                    ag_wait(color, s, j)
-                    if s > 0:
-                        ag_start(color, s - 1, j)
-
-            at_stage(t, LAG * (8 - s), gather)
+            at_stage(t, 1 + DUE[s], reduce)
+
+        def taps(j):
+            for color in range(2):
+                one_tap(j, xts[color], ycats[color], grads[color], widths[color])
+
+        at_stage(t, 0, taps)
         return carry
 
     cnt_start(0)
-    lax.fori_loop(0, chunks + 8 * LAG, tick, 0)
+    lax.fori_loop(0, 1 + chunks + DUE[-1], tick, 0)
 
     def drain(j, carry):
         for color in range(2):
@@ -390,8 +357,8 @@
             cnt_copy(s, k, m, far, device).wait_send()
 
 
-def summed_moments(n_gx, n_gy, roi_counts, anchor_counts, mask_g, rpn_g, mask_mo, rpn_mo):
-    chunks, chunk, chans = mask_g.shape
+def summed_moments(n_gx, n_gy, widths, steps, roi_counts, anchor_counts, fields, moments):
+    chunks, chunk, chans = moments[0].shape
     sizes = ((2, n_gx // 2, 2, n_gy // 2), (2, 2, n_gx // 2, n_gy // 2))
     smem, vmem = pl.BlockSpec(memory_space=pltpu.SMEM), pl.BlockSpec(memory_space=pltpu.VMEM)
     hbm = pl.BlockSpec(memory_space=pl.ANY)
@@ -405,28 +372,75 @@
             sems.append(pltpu.SemaphoreType.DMA((chunks, max(size - 1, 1))))
     piece = b
     small = [pltpu.SemaphoreType.DMA((max(size - 1, 1),)) for size in sizes[0]]
-    out = jax.ShapeDtypeStruct(mask_g.shape, jnp.float32)
+    out = jax.ShapeDtypeStruct(moments[0].shape, jnp.float32)
+    xts, ycats = [], []
+    for color in range(2):
+        images, depth, _ = fields[2 * color].shape
+        padded = -(-depth // 128) * 128
+        xts.append(pltpu.VMEM((images, chans, padded), jnp.bfloat16))
+        ycats.append(pltpu.VMEM((3, images, padded + 2 * widths[color], chans), jnp.bfloat16))
     return pl.pallas_call(
-        functools.partial(sum_kernel, n_gx, n_gy),
+        functools.partial(sum_kernel, n_gx, n_gy, widths, steps),
         out_shape=(out, out),
-        in_specs=[smem, smem, vmem, vmem, hbm, hbm],
+        in_specs=[smem, smem] + [vmem] * 4 + [hbm] * 2,
         out_specs=(vmem, vmem),
         scratch_shapes=[
-            pltpu.VMEM((2, chunks, chunk, chans), jnp.float32),
             pltpu.VMEM((2, chunks, piece, chans), jnp.float32),
             pltpu.SemaphoreType.DMA((2, chunks)),
             pltpu.VMEM((5, 16, 128), jnp.float32),
             pltpu.VMEM((4, widest, 16, 128), jnp.float32),
         ]
+        + xts
+        + ycats
+        + [pltpu.VMEM(moments[0].shape, jnp.float32)] * 2
         + landing
         + small
         + small
         + sems * 4,
         compiler_params=pltpu.CompilerParams(
-            collective_id=0, has_side_effects=True, vmem_limit_bytes=40 * 2**20
+            collective_id=0, has_side_effects=True, vmem_limit_bytes=43 * 2**20
         ),
-        name="sum_and_share",
-    )(roi_counts, anchor_counts, mask_g, rpn_g, mask_mo, rpn_mo)
+        name="grads_and_sum",
+    )(roi_counts, anchor_counts, *fields, *moments)
+
+
+def finish_kernel(w0, w1, m0, m1, nw0, nw1, nm0, nm1, s0, s1, m_sem, w_sem):
+    copies = []
+    for i, (m, out) in enumerate(((m0, nm0), (m1, nm1))):
+        copies.append(pltpu.make_async_copy(m, out, m_sem.at[i]))
+    for copy in copies:
+        copy.start()
+    rows = w0.shape[0]
+    parts = w_sem.shape[1]
+    step = rows // parts
+    for i, (w, m, s, out) in enumerate(((w0, m0, s0, nw0), (w1, m1, s1, nw1))):
+        for k in range(parts):
+            at = pl.ds(k * step, step)
+            s[at, :] = w[at, :] - 0.02 * m[at, :]
+            copy = pltpu.make_async_copy(s.at[at, :], out.at[at, :], w_sem.at[i, k])
+            copy.start()
+            copies.append(copy)
+    for copy in copies:
+        copy.wait()
+
+
+def finish(weights, moments):
+    out = jax.ShapeDtypeStruct(weights[0].shape, jnp.float32)
+    vmem, hbm = pl.BlockSpec(memory_space=pltpu.VMEM), pl.BlockSpec(memory_space=pl.ANY)
+    return pl.pallas_call(
+        finish_kernel,
+        out_shape=(out,) * 4,
+        in_specs=[vmem] * 4,
+        out_specs=(hbm,) * 4,
+        scratch_shapes=[
+            pltpu.VMEM(weights[0].shape, jnp.float32),
+            pltpu.VMEM(weights[0].shape, jnp.float32),
+            pltpu.SemaphoreType.DMA((2,)),
+            pltpu.SemaphoreType.DMA((2, 3)),
+        ],
+        compiler_params=pltpu.CompilerParams(vmem_limit_bytes=16 * 2**20),
+        name="finish",
+    )(*weights, *moments)
 
 
 def on_device(
@@ -443,19 +457,23 @@
     mask_moment,
     rpn_moment,
 ):
-    mask_g, rpn_g = local_grads(roi_counts, mask_feats, mask_cot, rpn_feats, rpn_cot)
-    new_mask, new_rpn = summed_moments(
+    images, slots, side, _, chans = mask_feats.shape
+    grid_cols = rpn_feats.shape[2]
+    fields = [v.transpose(0, 2, 3, 1, 4).reshape(images, -1, chans) for v in (mask_feats, mask_cot)]
+    fields += [v.reshape(images, -1, chans) for v in (rpn_feats, rpn_cot)]
+    taps = (TAPS, mask_moment.shape[0] // TAPS, chans)
+    moments = summed_moments(
         n_gx,
         n_gy,
+        (side * slots, grid_cols),
+        (slots, 1),
         roi_counts,
         anchor_counts,
-        mask_g,
-        rpn_g,
-        mask_moment.reshape(mask_g.shape),
-        rpn_moment.reshape(rpn_g.shape),
+        fields,
+        (mask_moment.reshape(taps), rpn_moment.reshape(taps)),
     )
-    new_mask, new_rpn = new_mask.reshape(mask_moment.shape), new_rpn.reshape(rpn_moment.shape)
-    return (mask_weight - 0.02 * new_mask, rpn_weight - 0.02 * new_rpn, new_mask, new_rpn)
+    moments = [m.reshape(mask_moment.shape) for m in moments]
+    return tuple(finish((mask_weight, rpn_weight), moments))
 
 
 def solution(mesh):

time: 90.4 us -> 74.6 us (0.83)
  Pallas kernels: 75.7 us -> 66.8 us
  local copies, waits for them, and re-layouts: 11 us -> 6.96 us
  other arithmetic: 2.82 us -> 0 us
    pallas_call x2, Pallas kernels: 75.7 us -> 66.8 us  [the longest x1 63.1 us: summed_moments(): pl.pallas_call(functools.partial(sum_kernel, n_gx, n_gy, widths, steps),...]
    unnamed x22 -> x16, local copies, waits for them, and re-layouts: 11 us -> 6.96 us
    sub x1 -> x0, other arithmetic: 2.82 us -> none  [on_device(): rpn_weight - 0.02 * new_rpn]
where the time goes in v2:
time: 74.6 us; the launch traced here: 74.4 us
  Pallas kernels  66.8 us (90%)
  local copies, waits for them, and re-layouts  6.96 us (9%)
    pallas_call x1, Pallas kernels, summed_moments(): pl.pallas_call(functools.partial(sum_kernel, n_gx, n_gy, widths, steps),...  63.1 us
    unnamed x16, local copies, waits for them, and re-layouts  6.96 us
    pallas_call x1, Pallas kernels, finish(): pl.pallas_call(finish_kernel, out_shape=(out,) * 4, in_specs=[vmem] * 4,...  3.69 us

profile of v2, /device:TPU:1, one launch (start us, length us, event | category | flops | bytes accessed | tf_op | source)
XLA Modules:
  0.0 74.4 jit_solution(13749386091897639629)
XLA Ops:
  0.6 0.0 copy-start.2
  0.6 1.4 %copy-done.2 = bf16[2,8,14,14,256]{4,1,3,2,0:T(8,128)(2,1)S(1)} copy-done((bf16[2,8,14,14,256]{4,1,3,2,0:T(8,128)(2,1)S(1)}, bf16[2,8,14,14,256]{4,1,3,2,0:T(8,128)(2,1)}, u32[]{:S(2)}) %copy-start.2) | copy-done | bytes 1605656
  2.1 0.0 copy-start.3
  2.1 1.4 %copy-done.3 = bf16[2,8,14,14,256]{4,1,3,2,0:T(8,128)(2,1)S(1)} copy-done((bf16[2,8,14,14,256]{4,1,3,2,0:T(8,128)(2,1)S(1)}, bf16[2,8,14,14,256]{4,1,3,2,0:T(8,128)(2,1)}, u32[]{:S(2)}) %copy-start.3) | copy-done | bytes 1605656
  3.5 0.0 copy-start.4
  3.5 1.4 %copy-done.4 = bf16[2,48,32,256]{3,2,1,0:T(8,128)(2,1)S(1)} copy-done((bf16[2,48,32,256]{3,2,1,0:T(8,128)(2,1)S(1)}, bf16[2,48,32,256]{3,2,1,0:T(8,128)(2,1)}, u32[]{:S(2)}) %copy-start.4) | copy-done | bytes 1572888
  4.9 0.0 copy-start.5
  4.9 1.4 %copy-done.5 = bf16[2,48,32,256]{3,2,1,0:T(8,128)(2,1)S(1)} copy-done((bf16[2,48,32,256]{3,2,1,0:T(8,128)(2,1)S(1)}, bf16[2,48,32,256]{3,2,1,0:T(8,128)(2,1)}, u32[]{:S(2)}) %copy-start.5) | copy-done | bytes 1572888
  6.3 0.0 copy-start.6
  6.3 0.7 copy-done.6
  6.9 0.0 copy-start.7
  6.9 0.7 copy-done.7
  7.6 0.0 copy-start
  7.6 0.0 copy-start.1
  7.6 63.1 %grads_and_sum.1 = (f32[9,256,256]{2,1,0:T(8,128)S(1)}, f32[9,256,256]{2,1,0:T(8,128)S(1)}) custom-call(s32[2]{0:T(128)S(1)} %copy-done.6, s32[2]{0:T(128)S(1)} %copy-done.7, bf16[2,1568,256]{2,1,0:T(8,128)(2,1)S(1)} %bitcast.14, bf16[2,1568,256]{2,1,0:T(8,128)(2,1)S(1)} %bitcast.15, bf16[2,1536,256]{2,1,0:T(8,128)(2,1)S(1)} %bitcast.16, ...), custom_call_target="tpu_custom_call" | custom-call | tf_op jit(solution)/shard_map/grads_and_sum/pallas_call | solution.py:382
  70.7 0.0 copy-done
  70.7 0.0 copy-done.1
  70.7 3.7 %finish.1 = (f32[2304,256]{1,0:T(8,128)}, f32[2304,256]{1,0:T(8,128)}, f32[2304,256]{1,0:T(8,128)}, f32[2304,256]{1,0:T(8,128)}) custom-call(f32[2304,256]{1,0:T(8,128)S(1)} %copy-done, f32[2304,256]{1,0:T(8,128)S(1)} %copy-done.1, f32[2304,256]{1,0:T(8,128)S(1)} %bitcast.12, f32[2304,256]{1,0:T(8,128)S(1)} %bitcast.13), custom_call_target="tpu_custom_call" | custom-call | tf_op jit(solution)/shard_map/finish/pallas_call | solution.py:430
Async XLA Ops:
  0.6 1.4 %copy-start.2 = (bf16[2,8,14,14,256]{4,1,3,2,0:T(8,128)(2,1)S(1)}, bf16[2,8,14,14,256]{4,1,3,2,0:T(8,128)(2,1)}, u32[]{:S(2)}) copy-start(bf16[2,8,14,14,256]{4,1,3,2,0:T(8,128)(2,1)} %param.10) | copy-start | bytes 4816900
  2.1 1.4 %copy-start.3 = (bf16[2,8,14,14,256]{4,1,3,2,0:T(8,128)(2,1)S(1)}, bf16[2,8,14,14,256]{4,1,3,2,0:T(8,128)(2,1)}, u32[]{:S(2)}) copy-start(bf16[2,8,14,14,256]{4,1,3,2,0:T(8,128)(2,1)} %param.11) | copy-start | bytes 4816900
  3.5 1.4 %copy-start.4 = (bf16[2,48,32,256]{3,2,1,0:T(8,128)(2,1)S(1)}, bf16[2,48,32,256]{3,2,1,0:T(8,128)(2,1)}, u32[]{:S(2)}) copy-start(bf16[2,48,32,256]{3,2,1,0:T(8,128)(2,1)} %param.13) | copy-start | bytes 4718596
  4.9 1.4 %copy-start.5 = (bf16[2,48,32,256]{3,2,1,0:T(8,128)(2,1)S(1)}, bf16[2,48,32,256]{3,2,1,0:T(8,128)(2,1)}, u32[]{:S(2)}) copy-start(bf16[2,48,32,256]{3,2,1,0:T(8,128)(2,1)} %param.14) | copy-start | bytes 4718596
  6.3 0.7 copy-start.6
  6.9 0.7 copy-start.7
  7.6 63.1 %copy-start = (f32[2304,256]{1,0:T(8,128)S(1)}, f32[2304,256]{1,0:T(8,128)}, u32[]{:S(2)}) copy-start(f32[2304,256]{1,0:T(8,128)} %w0.1) | copy-start | bytes 7077892
  7.6 63.1 %copy-start.1 = (f32[2304,256]{1,0:T(8,128)S(1)}, f32[2304,256]{1,0:T(8,128)}, u32[]{:S(2)}) copy-start(f32[2304,256]{1,0:T(8,128)} %w1.1) | copy-start | bytes 7077892
